TPU v7x, 32 devices: a whole 2x2x4 slice. The times are simulated.
32 devices in a mesh: groups: 2 (over y), seq: 4 (over z), head: 4 (over x, core).
Axes of the slice: x: 2, y: 2, z: 4, core: 2. Of those that a mesh axis runs over, the one named last changes fastest.
Arguments:
- queries: bfloat16 [2048, 8192], P(('groups', 'seq'), 'head'), parts along dimension 0, may hold values from -16 to 16
- keys: bfloat16 [2048, 1024], P(('groups', 'seq'), 'head'), parts along dimension 0, may hold values from -16 to 16
- values: bfloat16 [2048, 1024], P(('groups', 'seq'), 'head'), parts along dimension 0, may hold values from -6 to 6
- prompt_len: int32 [2], P('groups'), parts along dimension 0, may hold values from 256 to 1024
- page_dest: int32 [8, 2], P('groups'), parts along dimension 0, may hold values from 0 to 3, all different within a row; in each aligned block of 4 rows (0 to 3, 4 to 7, ...) at most 4 rows name the same one
Outputs:
- attended: bfloat16 [2048, 8192], P(('groups', 'seq'), 'head'), parts along dimension 0
- decode_page_cache: bfloat16 [32, 128, 2048], P(('groups', 'seq'), None, 'head'), parts along dimension 0
There are 2 independent parts, one for each index of `groups`. A program takes and returns all parts, laid end to end along the dimension named above; each array names one. Nothing has to cross between parts.
Inputs may be any that keep to these rules, and one draw needn't show every extreme that they name: `page_dest`: row s names the decode devices of the 2 pages of tokens s * 256 to (s + 1) * 256 - 1, all different within a row; no device is named more than 4 times in all, and some device exactly 4 times.
All inputs are finite; a program needn't handle non-finite values.
Results may differ from a plain program's by a relative error of at most 0.005.
Values may be sent and summed in bfloat16 or wider, within the bound.
A program may use at most 64 MiB of HBM per device.

v0:
```python
import math
import jax
import jax.numpy as jnp
from jax import lax
from jax.sharding import PartitionSpec as P

HEAD_SIZE = 128
PAGE_TOKENS = 128
NEG_FILL = -1e30


def blank_state(kv_heads, group_size, query_count):
    return (
        jnp.full((kv_heads, group_size, query_count), NEG_FILL, jnp.float32),
        jnp.zeros((kv_heads, group_size, query_count), jnp.float32),
        jnp.zeros((kv_heads, group_size, query_count, HEAD_SIZE), jnp.float32),
    )


def attend_block(
    query_state, query_block, query_pos, key_block, value_block, block_start, prompt_end
):
    key_count = key_block.shape[0]
    kv_heads = key_block.shape[1] // HEAD_SIZE
    keys_split = key_block.reshape(key_count, kv_heads, HEAD_SIZE)
    values_split = value_block.reshape(key_count, kv_heads, HEAD_SIZE)
    scores = jnp.einsum(
        "rkgd,pkd->kgrp", query_block, keys_split, preferred_element_type=jnp.float32
    )
    scores = scores * (1.0 / math.sqrt(HEAD_SIZE))
    key_pos = block_start + jnp.arange(key_count, dtype=jnp.int32)
    allowed = (key_pos[None, :] <= query_pos[:, None]) & (key_pos[None, :] < prompt_end)
    scores = jnp.where(allowed, scores, NEG_FILL)
    old_max = query_state[0]
    new_max = jnp.maximum(old_max, jnp.max(scores, axis=-1))
    weights = jnp.where(allowed, jnp.exp(scores - new_max[..., None]), 0.0)
    factor = jnp.exp(old_max - new_max)
    denominator = query_state[1] * factor + jnp.sum(weights, axis=-1)
    accumulated = query_state[2] * factor[..., None] + jnp.einsum(
        "kgrp,pkd->kgrd",
        weights.astype(jnp.bfloat16),
        values_split,
        preferred_element_type=jnp.float32,
    )
    return (new_max, denominator, accumulated)


def finish(query_state, query_pos, prompt_end):
    query_live = query_pos < prompt_end
    safe_total = jnp.where(query_live[None, None, :], query_state[1], 1.0)
    result = jnp.where(query_live[None, None, :, None], query_state[2] / safe_total[..., None], 0.0)
    query_count = query_pos.shape[0]
    return result.transpose(2, 0, 1, 3).reshape(query_count, -1).astype(jnp.bfloat16)


def join_pages(key_rows, value_rows):
    page_count = key_rows.shape[0] // PAGE_TOKENS
    kv_heads = key_rows.shape[1] // HEAD_SIZE
    stacked = jnp.stack(
        (
            key_rows.reshape(page_count, PAGE_TOKENS, kv_heads, HEAD_SIZE),
            value_rows.reshape(page_count, PAGE_TOKENS, kv_heads, HEAD_SIZE),
        ),
        axis=3,
    )
    return stacked.reshape(page_count, PAGE_TOKENS, 2 * key_rows.shape[1])


def slot_pages(page_dest, owner, slots):
    flat_dest = page_dest.reshape(-1)
    page_order = jnp.arange(flat_dest.shape[0], dtype=jnp.int32)
    same_dest = flat_dest[:, None] == flat_dest[None, :]
    dest_rank = jnp.sum(same_dest & (page_order[None, :] < page_order[:, None]), axis=1)
    matched = (flat_dest[:, None] == owner) & (
        dest_rank[:, None] == jnp.arange(slots, dtype=jnp.int32)[None, :]
    )
    page_index = jnp.sum(jnp.where(matched, page_order[:, None], 0), axis=0)
    present = jnp.any(matched, axis=0)
    return (flat_dest, page_index, present)


def place_pages(stored, key_block, value_block, block_start, prompt_end, page_index, present):
    key_pos = block_start + jnp.arange(key_block.shape[0], dtype=jnp.int32)
    token_present = (key_pos < prompt_end)[:, None]
    block_pages = join_pages(
        jnp.where(token_present, key_block, 0), jnp.where(token_present, value_block, 0)
    )
    page_count = block_pages.shape[0]
    local_index = page_index - block_start // PAGE_TOKENS
    inside = present & (local_index >= 0) & (local_index < page_count)
    picked = block_pages[jnp.clip(local_index, 0, page_count - 1)]
    return jnp.where(inside[:, None, None], picked, stored)


def local(queries, keys, values, prompt_len, page_dest):
    shard_rows = queries.shape[0]
    kv_width = keys.shape[1]
    kv_heads = kv_width // HEAD_SIZE
    group_size = queries.shape[1] // kv_width
    seq_index = lax.axis_index("seq")
    prompt_end = prompt_len[0]
    per_device = page_dest.shape[1]
    slots = 2 * per_device
    flat_dest, page_index, present = slot_pages(page_dest, seq_index, slots)
    own_rows = seq_index * shard_rows + jnp.arange(shard_rows, dtype=jnp.int32)
    query_parts = (queries,)
    positions = (own_rows,)
    shaped = tuple(
        (
            part_rows.reshape(part_rows.shape[0], kv_heads, group_size, HEAD_SIZE)
            for part_rows in query_parts
        )
    )
    states = tuple(
        (blank_state(kv_heads, group_size, part_rows.shape[0]) for part_rows in query_parts)
    )
    page_store = jnp.zeros((slots, PAGE_TOKENS, 2 * kv_width), jnp.bfloat16)
    key_piece = lax.all_gather(keys, "seq", axis=0, tiled=True)
    value_piece = lax.all_gather(values, "seq", axis=0, tiled=True)
    block_count = key_piece.shape[0] // shard_rows
    per_step = max(1, min(block_count, 512 // shard_rows))
    while block_count % per_step:
        per_step -= 1
    step_rows = per_step * shard_rows
    steps_count = block_count // per_step
    key_blocks = key_piece.reshape(steps_count, step_rows, kv_width)
    value_blocks = value_piece.reshape(steps_count, step_rows, kv_width)

    def one_block(inner_carry, block_item):
        block_states, stored = inner_carry
        key_block, value_block, number = block_item
        block_start = number * step_rows
        updated = []
        for query_state, query_block, query_pos in zip(block_states, shaped, positions):
            needed = block_start <= jnp.minimum(query_pos[-1], prompt_end - 1)
            updated.append(
                lax.cond(
                    needed,
                    lambda kept: attend_block(
                        kept,
                        query_block,
                        query_pos,
                        key_block,
                        value_block,
                        block_start,
                        prompt_end,
                    ),
                    lambda kept: kept,
                    query_state,
                )
            )
        stored = place_pages(
            stored, key_block, value_block, block_start, prompt_end, page_index, present
        )
        return ((tuple(updated), stored), None)

    result, unused = lax.scan(
        one_block,
        (states, page_store),
        (key_blocks, value_blocks, jnp.arange(steps_count, dtype=jnp.int32)),
    )
    final_states, stored = result
    outputs = [
        finish(query_state, query_pos, prompt_end)
        for query_state, query_pos in zip(final_states, positions)
    ]
    attended = outputs[0]
    return (attended, stored)


def solution(mesh):
    return jax.shard_map(
        local,
        mesh=mesh,
        in_specs=(
            P(("groups", "seq"), "head"),
            P(("groups", "seq"), "head"),
            P(("groups", "seq"), "head"),
            P("groups"),
            P("groups", None),
        ),
        out_specs=(P(("groups", "seq"), "head"), P(("groups", "seq"), None, "head")),
        check_vma=False,
    )
```

profile of v0, /device:TPU:26, one launch (start us, length us, event | category | flops | bytes accessed | tf_op | source)
XLA Modules:
  0.0 76.9 jit_solution(3035175965505265752)
XLA Ops:
  1.3 0.7 slice.5
  2.7 0.8 copy.34
  3.4 0.1 broadcast_in_dim_reshape.2
  3.5 0.2 convert_reduce_fusion
  3.7 0.1 fusion.20
  3.8 0.1 select_reduce_fusion
  4.0 16.3 %all_gather.6 = bf16[1024,256]{1,0:T(8,128)(2,1)} all-gather(bf16[256,256]{1,0:T(8,128)(2,1)} %param.10), channel_id=1, replica_groups=mesh['groups'=2,'seq'=4,'head'=4] {'seq'}, dimensions={0}, use_global_device_ids=true | all-gather | bytes 655360 | tf_op jit(solution)/shard_map/all_gather | solution.py:118
  20.3 16.4 %all_gather.7 = bf16[1024,256]{1,0:T(8,128)(2,1)} all-gather(bf16[256,256]{1,0:T(8,128)(2,1)} %param.11), channel_id=1, replica_groups=mesh['groups'=2,'seq'=4,'head'=4] {'seq'}, dimensions={0}, use_global_device_ids=true | all-gather | bytes 655360 | tf_op jit(solution)/shard_map/all_gather | solution.py:119
  36.7 1.5 %copy.33 = bf16[256,2048]{0,1:T(8,128)(2,1)S(1)} copy(bf16[256,2048]{1,0:T(8,128)(2,1)} %param.9) | data formatting | bytes 2097152 | tf_op args[0]
  38.2 0.7 copy.35
  38.9 1.6 %broadcast_in_dim.106 = f32[2,8,256,128]{3,2,1,0:T(8,128)} broadcast(f32[]{:T(128)} %constant.102.clone.1), dimensions={} | broadcast | bytes 2097156 | tf_op jit(solution)/shard_map/broadcast_in_dim | solution.py:16
  40.4 31.5 %while.20 = (s32[]{:T(128)}, f32[2,8,256]{2,1,0:T(8,128)S(1)}, f32[2,8,256]{2,1,0:T(8,128)S(1)}, f32[2,8,256,128]{3,2,1,0:T(8,128)}, bf16[4,128,512]{1,2,0:T(8,1...) while((s32[]{:T(128)}, f32[2,8,256]{2,1,0:T(8,128)S(1)}, ...), condition=%wide.region_8.9_spmd.clone, body=%wide.region_3.8_spmd.clone.sunk | while | flops 1103377152 | bytes 57424572 | solution.py:157
  40.4 0.7 dynamic_slice.31
  41.9 0.7 add_compare_fusion.2
  42.5 1.1 %constant_dynamic-slice_fusion.3 = (bf16[1,512,256]{2,1,0:T(8,128)(2,1)S(1)}, bf16[1,512,256]{2,1,0:T(8,128)(2,1)S(1)}) fusion(bf16[2,512,256]{2,1,0:T(8,128)(2,1)} %get-tuple-element.556, s32[]{:T(128)S(6)} %copy.67, bf16[2,512,256]{2,1,0:T(8,128)(2,1)} %get-tuple-element.555), kind=kLoop, calls=%fused_computation.31.clone.1 | loop fusion | bytes 1048580 | tf_op jit(solution)/shard_map/while/body/jit(dynamic_index_in_dim)/dynamic_slice | solution.py:157
  43.6 0.1 squeeze.31
  43.7 0.1 squeeze.32
  43.8 1.1 %broadcast_select_fusion.4 = (bf16[4,128,2,1,128]{4,2,1,0,3:T(2,128)(2,1)S(1)}, bf16[4,128,2,1,128]{4,2,1,0,3:T(2,128)(2,1)S(1)}) fusion(bf16[4,128,2,1,128]{4,2,1,0,3:T(2,128)(2,1)S(1)} %squeeze.31, pred[4,128]{1,0:T(4,128)(4,1)S(1)} %add_compare_fusion.2, bf16[4,128,2,1,128]{4,2,1,0,3:T(2,128)(2,1)S(1)} %squeeze.32), kind=kLoop, calls=%fused_computation.25.clone.1 | loop fusion | flops 262144 | bytes 1049088 | tf_op jit(solution)/shard_map/while/body/eval_jaxpr/jit(_where)/select_n | solution.py:86
  44.9 0.7 pad_maximum_fusion.2
  45.6 0.4 copy.55
  46.1 0.6 gather_fusion
  46.7 0.2 select_select_fusion.2
  46.9 9.3 %conditional.3 = ((f32[2,8,256]{2,1,0:T(8,128)S(1)}, f32[2,8,256]{2,1,0:T(8,128)S(1)}, f32[2,8,256,128]{3,2,1,0:T(8,128)})) conditional(s32[]{:T(128)} %convert_element_type.41, (f32[2,8,256]{2,1,0:T(8,128)S(1)}, f32[2,8,256]{2,1,0:T(8,128)S(1)}, f32[2,8,256,128]{3,2,1,0:T(8,128)}) %tuple.62, (s32[]{:T(128)}, s32[]{:T(128)}, s32[]{:T(128)}, ...), branch_computations={%region_4.4_spmd, %region_5.7_spmd} | conditional | flops 1102325504 | bytes 49553512 | solution.py:137
  46.9 0.7 broadcast_compare_fusion
  47.6 0.2 compare_and_fusion
  47.8 0.1 reshape.144
  47.9 0.1 reshape.145
  47.9 0.0 copy-start
  48.0 1.4 %fusion.2 = (f32[2,8,256]{2,1,0:T(8,128)S(1)}, f32[2,512,256,8]{2,1,3,0:T(8,128)S(1)}) fusion(pred[256,512]{0,1:T(8,128)(4,1)S(1)} %compare_and_fusion, bf16[256,2,8,128]{3,0,2,1:T(8,128)(2,1)S(1)} %get-tuple-element.235, bf16[512,2,128,1]{2,1,0,3:T(2,128)(2,1)S(1)} %bitcast.45), kind=kOutput, calls=%fused_computation.4 | convolution fusion | flops 543158272 | bytes 9846784 | tf_op jit(solution)/shard_map/while/body/eval_jaxpr/cond/branch_1_fun/rkgd,pkd->kgrp/dot_general | solution.py:27
  49.4 2.0 %fusion.4 = f32[2,8,256]{2,1,0:T(8,128)S(1)} fusion(f32[2,512,256,8]{2,1,3,0:T(8,128)S(1)} %get-tuple-element.398, f32[2,8,256]{2,1,0:T(8,128)S(1)} %max.6, pred[256,512]{0,1:T(8,128)(4,1)S(1)} %compare_and_fusion), kind=kLoop, calls=%fused_computation.6 | loop fusion | flops 10481664 | bytes 8552448 | tf_op jit(solution)/shard_map/while/body/eval_jaxpr/cond/branch_1_fun/reduce_sum | solution.py:38
  51.4 0.0 copy-done
  51.4 3.4 %multiply_add_fusion = f32[2,8,256,128]{3,2,1,0:T(8,128)S(1)} fusion(f32[2,8,256,128]{3,2,1,0:T(8,128)S(1)} %copy-done, f32[2,512,256,8]{2,1,3,0:T(8,128)S(1)} %get-tuple-element.398, f32[2,8,256]{2,1,0:T(8,128)S(1)} %max.6, pred[256,512]{0,1:T(8,128)(4,1)S(1)} %compare_and_fusion, f32[2,8,256]{2,1,0:T(8,128)S(1)} %get-tuple-element.396, ...), kind=kOutput, calls=%fused_computation.9 | convolution fusion | flops 548405248 | bytes 13008896 | tf_op jit(solution)/shard_map/while/body/eval_jaxpr/cond/branch_1_fun/kgrp,pkd->kgrd/dot_general | solution.py:39
  54.8 0.0 copy-start.1
  54.9 1.3 %copy-done.1 = f32[2,8,256,128]{3,2,1,0:T(8,128)} copy-done((f32[2,8,256,128]{3,2,1,0:T(8,128)}, f32[2,8,256,128]{3,2,1,0:T(8,128)S(1)}, u32[]{:S(2)}) %copy-start.1) | copy-done | bytes 2097176 | tf_op jit(solution)/shard_map/while/body/eval_jaxpr/cond
  56.2 0.7 dynamic_slice.31
  57.6 0.7 add_compare_fusion.2
  58.3 1.1 %constant_dynamic-slice_fusion.3 = (bf16[1,512,256]{2,1,0:T(8,128)(2,1)S(1)}, bf16[1,512,256]{2,1,0:T(8,128)(2,1)S(1)}) fusion(bf16[2,512,256]{2,1,0:T(8,128)(2,1)} %get-tuple-element.556, s32[]{:T(128)S(6)} %copy.67, bf16[2,512,256]{2,1,0:T(8,128)(2,1)} %get-tuple-element.555), kind=kLoop, calls=%fused_computation.31.clone.1 | loop fusion | bytes 1048580 | tf_op jit(solution)/shard_map/while/body/jit(dynamic_index_in_dim)/dynamic_slice | solution.py:157
  59.4 0.1 squeeze.31
  59.5 0.1 squeeze.32
  59.5 1.1 %broadcast_select_fusion.4 = (bf16[4,128,2,1,128]{4,2,1,0,3:T(2,128)(2,1)S(1)}, bf16[4,128,2,1,128]{4,2,1,0,3:T(2,128)(2,1)S(1)}) fusion(bf16[4,128,2,1,128]{4,2,1,0,3:T(2,128)(2,1)S(1)} %squeeze.31, pred[4,128]{1,0:T(4,128)(4,1)S(1)} %add_compare_fusion.2, bf16[4,128,2,1,128]{4,2,1,0,3:T(2,128)(2,1)S(1)} %squeeze.32), kind=kLoop, calls=%fused_computation.25.clone.1 | loop fusion | flops 262144 | bytes 1049088 | tf_op jit(solution)/shard_map/while/body/eval_jaxpr/jit(_where)/select_n | solution.py:86
  60.6 0.7 pad_maximum_fusion.2
  61.4 0.4 copy.55
  61.8 0.6 gather_fusion
  62.5 0.2 select_select_fusion.2
  62.7 9.3 %conditional.3 = ((f32[2,8,256]{2,1,0:T(8,128)S(1)}, f32[2,8,256]{2,1,0:T(8,128)S(1)}, f32[2,8,256,128]{3,2,1,0:T(8,128)})) conditional(s32[]{:T(128)} %convert_element_type.41, (f32[2,8,256]{2,1,0:T(8,128)S(1)}, f32[2,8,256]{2,1,0:T(8,128)S(1)}, f32[2,8,256,128]{3,2,1,0:T(8,128)}) %tuple.62, (s32[]{:T(128)}, s32[]{:T(128)}, s32[]{:T(128)}, ...), branch_computations={%region_4.4_spmd, %region_5.7_spmd} | conditional | flops 1102325504 | bytes 49553512 | solution.py:137
  62.7 0.7 broadcast_compare_fusion
  63.4 0.2 compare_and_fusion
  63.6 0.1 reshape.144
  63.6 0.1 reshape.145
  63.7 0.0 copy-start
  63.7 1.4 %fusion.2 = (f32[2,8,256]{2,1,0:T(8,128)S(1)}, f32[2,512,256,8]{2,1,3,0:T(8,128)S(1)}) fusion(pred[256,512]{0,1:T(8,128)(4,1)S(1)} %compare_and_fusion, bf16[256,2,8,128]{3,0,2,1:T(8,128)(2,1)S(1)} %get-tuple-element.235, bf16[512,2,128,1]{2,1,0,3:T(2,128)(2,1)S(1)} %bitcast.45), kind=kOutput, calls=%fused_computation.4 | convolution fusion | flops 543158272 | bytes 9846784 | tf_op jit(solution)/shard_map/while/body/eval_jaxpr/cond/branch_1_fun/rkgd,pkd->kgrp/dot_general | solution.py:27
  65.2 2.0 %fusion.4 = f32[2,8,256]{2,1,0:T(8,128)S(1)} fusion(f32[2,512,256,8]{2,1,3,0:T(8,128)S(1)} %get-tuple-element.398, f32[2,8,256]{2,1,0:T(8,128)S(1)} %max.6, pred[256,512]{0,1:T(8,128)(4,1)S(1)} %compare_and_fusion), kind=kLoop, calls=%fused_computation.6 | loop fusion | flops 10481664 | bytes 8552448 | tf_op jit(solution)/shard_map/while/body/eval_jaxpr/cond/branch_1_fun/reduce_sum | solution.py:38
  67.2 0.0 copy-done
  67.2 3.4 %multiply_add_fusion = f32[2,8,256,128]{3,2,1,0:T(8,128)S(1)} fusion(f32[2,8,256,128]{3,2,1,0:T(8,128)S(1)} %copy-done, f32[2,512,256,8]{2,1,3,0:T(8,128)S(1)} %get-tuple-element.398, f32[2,8,256]{2,1,0:T(8,128)S(1)} %max.6, pred[256,512]{0,1:T(8,128)(4,1)S(1)} %compare_and_fusion, f32[2,8,256]{2,1,0:T(8,128)S(1)} %get-tuple-element.396, ...), kind=kOutput, calls=%fused_computation.9 | convolution fusion | flops 548405248 | bytes 13008896 | tf_op jit(solution)/shard_map/while/body/eval_jaxpr/cond/branch_1_fun/kgrp,pkd->kgrd/dot_general | solution.py:39
  70.6 0.0 copy-start.1
  70.6 1.3 %copy-done.1 = f32[2,8,256,128]{3,2,1,0:T(8,128)} copy-done((f32[2,8,256,128]{3,2,1,0:T(8,128)}, f32[2,8,256,128]{3,2,1,0:T(8,128)S(1)}, u32[]{:S(2)}) %copy-start.1) | copy-done | bytes 2097176 | tf_op jit(solution)/shard_map/while/body/eval_jaxpr/cond
  72.0 2.0 %fusion.17 = bf16[256,2,8,128]{3,0,2,1:T(8,128)(2,1)S(1)} fusion(f32[2,8,256,128]{3,2,1,0:T(8,128)} %get-tuple-element.262, f32[2,8,256]{2,1,0:T(8,128)S(1)} %broadcast_select_fusion.2, pred[256]{0:T(512)(128)(4,1)S(1)} %broadcast_compare_fusion.1), kind=kLoop, calls=%fused_computation.35 | loop fusion | flops 1572864 | bytes 3162368 | tf_op jit(solution)/shard_map/convert_element_type | solution.py:53
  74.0 0.7 copy.36
  74.7 1.2 %copy.53 = bf16[32,8,16,128]{3,1,2,0:T(8,128)(2,1)} copy(bf16[32,8,16,128]{3,2,1,0:T(8,128)(2,1)S(1)} %bitcast.47) | data formatting | bytes 2097152
  75.9 1.0 %copy.37 = bf16[4,128,512]{2,1,0:T(8,128)(2,1)} copy(bf16[4,128,512]{1,2,0:T(8,128)(2,1)S(1)} %get-tuple-element.363) | data formatting | bytes 1048576
  (26 shorter events, 0.1 us)
Async XLA Ops:
  47.9 3.5 %copy-start = (f32[2,8,256,128]{3,2,1,0:T(8,128)S(1)}, f32[2,8,256,128]{3,2,1,0:T(8,128)}, u32[]{:S(2)}) copy-start(f32[2,8,256,128]{3,2,1,0:T(8,128)} %get-tuple-element.237) | copy-start | bytes 6291460 | tf_op jit(solution)/shard_map/while/body/eval_jaxpr/cond
  54.8 1.4 %copy-start.1 = (f32[2,8,256,128]{3,2,1,0:T(8,128)}, f32[2,8,256,128]{3,2,1,0:T(8,128)S(1)}, u32[]{:S(2)}) copy-start(f32[2,8,256,128]{3,2,1,0:T(8,128)S(1)} %multiply_add_fusion) | copy-start | bytes 6291460 | tf_op jit(solution)/shard_map/while/body/eval_jaxpr/cond
  63.7 3.5 %copy-start = (f32[2,8,256,128]{3,2,1,0:T(8,128)S(1)}, f32[2,8,256,128]{3,2,1,0:T(8,128)}, u32[]{:S(2)}) copy-start(f32[2,8,256,128]{3,2,1,0:T(8,128)} %get-tuple-element.237) | copy-start | bytes 6291460 | tf_op jit(solution)/shard_map/while/body/eval_jaxpr/cond
  70.6 1.4 %copy-start.1 = (f32[2,8,256,128]{3,2,1,0:T(8,128)}, f32[2,8,256,128]{3,2,1,0:T(8,128)S(1)}, u32[]{:S(2)}) copy-start(f32[2,8,256,128]{3,2,1,0:T(8,128)S(1)} %multiply_add_fusion) | copy-start | bytes 6291460 | tf_op jit(solution)/shard_map/while/body/eval_jaxpr/cond
where the time goes:
time: 77.3 us; the launch traced here: 76.9 us
  blocking collectives  32.7 us (42%)
  local copies, waits for them, and re-layouts  17.1 us (22%)
  other arithmetic  13.6 us (18%)
  matrix products  9.64 us (12%)
  between operations  2.06 us (3%)
  loops' own time  1.84 us (2%)
    all_gather x1, blocking collectives, local(): value_piece = lax.all_gather(values, 'seq', axis=0, tiled=True)  16.4 us
    all_gather x1, blocking collectives, local(): key_piece = lax.all_gather(keys, 'seq', axis=0, tiled=True)  16.3 us
    dot_general x2, matrix products, attend_block(): jnp.einsum('kgrp,pkd->kgrd', weights.astype(jnp.bfloat16), values_split,...  6.81 us
    unnamed x5, local copies, waits for them, and re-layouts  5.16 us
    reduce_sum x2, other arithmetic, attend_block(): denominator = query_state[1] * factor + jnp.sum(weights, axis=-1)  4.01 us
    dynamic_slice x4, local copies, waits for them, and re-layouts, local(): lax.scan(one_block, (states, page_store), (key_blocks, value_blocks, jnp....  3.47 us
    dot_general x2, matrix products, attend_block(): jnp.einsum('rkgd,pkd->kgrp', query_block, keys_split, preferred_element_t...  2.83 us
    cond x10, local copies, waits for them, and re-layouts  2.71 us

commit v1 on v0

--- a/solution.py
+++ b/solution.py
@@ -115,8 +115,11 @@
         (blank_state(kv_heads, group_size, part_rows.shape[0]) for part_rows in query_parts)
     )
     page_store = jnp.zeros((slots, PAGE_TOKENS, 2 * kv_width), jnp.bfloat16)
-    key_piece = lax.all_gather(keys, "seq", axis=0, tiled=True)
-    value_piece = lax.all_gather(values, "seq", axis=0, tiled=True)
+    key_piece, value_piece = jnp.split(
+        lax.all_gather(jnp.concatenate([keys, values], axis=1), "seq", axis=0, tiled=True),
+        [keys.shape[1]],
+        axis=1,
+    )
     block_count = key_piece.shape[0] // shard_rows
     per_step = max(1, min(block_count, 512 // shard_rows))
     while block_count % per_step:

time: 77.3 us -> 85.9 us (1.11); the launches traced: 76.9 us -> 84.5 us
  blocking collectives: 32.7 us -> 0 us
  waiting for transfers between devices: 0 us -> 23.3 us
  between operations: 2.06 us -> 15.4 us
  local copies, waits for them, and re-layouts: 17.1 us -> 19.2 us
  other arithmetic: 13.6 us -> 15.3 us
    all_gather x2 -> x0, blocking collectives: 32.7 us -> none  [the longest x1 16.4 us: local(): value_piece = lax.all_gather(values, 'seq', axis=0, tiled=True)]
    all_gather x0 -> x1, waiting for transfers between devices: none -> 23.3 us  [local(): lax.all_gather(jnp.concatenate([keys, values], axis=1), 'seq', axis=0, ti...]
    split x0 -> x1, local copies, waits for them, and re-layouts: none -> 2.23 us  [local(): jnp.split(lax.all_gather(jnp.concatenate([keys, values], axis=1), 'seq',...]
    concatenate x0 -> x1, other arithmetic: none -> 1.69 us  [local(): jnp.concatenate([keys, values], axis=1)]
  transfers between devices with their start and end apart: 0 -> 1, of which waited for: 0 -> 1; matrix products, arithmetic and copies ran while one was open for 0% -> 5% of each run, Pallas kernels for 0% -> 0%
where the time goes in v1:
time: 85.9 us; the launch traced here: 84.5 us
  waiting for transfers between devices  23.3 us (27%)
  local copies, waits for them, and re-layouts  19.2 us (22%)
  between operations  15.4 us (18%)
  other arithmetic  15.3 us (18%)
  matrix products  9.64 us (11%)
  loops' own time  1.7 us (2%)
    all_gather x1, waiting for transfers between devices, local(): lax.all_gather(jnp.concatenate([keys, values], axis=1), 'seq', axis=0, ti...  23.3 us
    dot_general x2, matrix products, attend_block(): jnp.einsum('kgrp,pkd->kgrd', weights.astype(jnp.bfloat16), values_split,...  6.8 us
    unnamed x5, local copies, waits for them, and re-layouts  5.15 us
    reduce_sum x2, other arithmetic, attend_block(): denominator = query_state[1] * factor + jnp.sum(weights, axis=-1)  4.01 us
    dynamic_slice x4, local copies, waits for them, and re-layouts, local(): lax.scan(one_block, (states, page_store), (key_blocks, value_blocks, jnp....  3.41 us
    dot_general x2, matrix products, attend_block(): jnp.einsum('rkgd,pkd->kgrp', query_block, keys_split, preferred_element_t...  2.83 us
    cond x10, local copies, waits for them, and re-layouts  2.71 us
    split x1, local copies, waits for them, and re-layouts, local(): jnp.split(lax.all_gather(jnp.concatenate([keys, values], axis=1), 'seq',...  2.23 us
  transfers between devices with their start and end apart: 1, of which 1 were waited for; matrix products, arithmetic and copies ran while one was open for 5% of the time, Pallas kernels for 0%

profile of v1, /device:TPU:26, one launch (start us, length us, event | category | flops | bytes accessed | tf_op | source)
XLA Modules:
  0.0 84.5 jit_solution(5130663248949104899)
XLA Ops:
  7.2 0.0 all-gather.2.cloned.1.call-start
  7.2 1.7 %pad_maximum_fusion.1 = bf16[256,512]{1,0:T(8,128)(2,1)} fusion(bf16[256,256]{1,0:T(8,128)(2,1)} %param.11, bf16[256,256]{1,0:T(8,128)(2,1)} %param.10), kind=kLoop, calls=%fused_computation.36 | loop fusion | flops 524288 | bytes 524288 | tf_op jit(solution)/shard_map/concatenate | solution.py:119
  8.9 0.0 all-gather.2.cloned.1.call-update
  9.6 0.6 slice.5
  10.2 0.8 copy.34
  10.9 0.1 broadcast_in_dim_reshape.2
  11.0 1.5 %copy.33 = bf16[256,2048]{0,1:T(8,128)(2,1)S(1)} copy(bf16[256,2048]{1,0:T(8,128)(2,1)} %param.9) | data formatting | bytes 2097152 | tf_op args[0]
  12.5 0.7 copy.35
  13.9 0.2 convert_reduce_fusion
  14.0 0.1 fusion.20
  14.2 0.1 select_reduce_fusion
  14.3 23.3 %all-gather.2.cloned.1.call-done = bf16[1024,512]{1,0:T(8,128)(2,1)} async-done(((bf16[256,512]{1,0:T(8,128)(2,1)}), bf16[1024,512]{1,0:T(8,128)(2,1)}) %all-gather.2.cloned.1.call-update) | async-done | bytes 1048592 | tf_op jit(solution)/shard_map/all_gather | solution.py:119
  37.5 2.2 %fusion.21 = (bf16[1024,256]{1,0:T(8,128)(2,1)}, bf16[1024,256]{1,0:T(8,128)(2,1)}) fusion(bf16[1024,512]{1,0:T(8,128)(2,1)} %all-gather.2.cloned.1.call-done), kind=kLoop, calls=%fused_computation.48 | loop fusion | bytes 2097152 | tf_op jit(solution)/shard_map/split | solution.py:118
  39.8 1.6 %broadcast_in_dim.106 = f32[2,8,256,128]{3,2,1,0:T(8,128)} broadcast(f32[]{:T(128)} %constant.102.clone.1), dimensions={} | broadcast | bytes 2097156 | tf_op jit(solution)/shard_map/broadcast_in_dim | solution.py:16
  41.4 31.3 %while.20 = (s32[]{:T(128)}, f32[2,8,256]{2,1,0:T(8,128)S(1)}, f32[2,8,256]{2,1,0:T(8,128)S(1)}, f32[2,8,256,128]{3,2,1,0:T(8,128)}, bf16[4,128,512]{1,2,0:T(8,1...) while((s32[]{:T(128)}, f32[2,8,256]{2,1,0:T(8,128)S(1)}, ...), condition=%wide.region_8.9_spmd.clone, body=%wide.region_3.8_spmd.clone.sunk | while | flops 1103377152 | bytes 57424572 | solution.py:160
  41.4 0.6 dynamic_slice.31
  42.7 0.7 add_compare_fusion.2
  43.4 1.1 %constant_dynamic-slice_fusion.3 = (bf16[1,512,256]{2,1,0:T(8,128)(2,1)S(1)}, bf16[1,512,256]{2,1,0:T(8,128)(2,1)S(1)}) fusion(bf16[2,512,256]{2,1,0:T(8,128)(2,1)} %get-tuple-element.558, s32[]{:T(128)S(6)} %copy.67, bf16[2,512,256]{2,1,0:T(8,128)(2,1)} %get-tuple-element.557), kind=kLoop, calls=%fused_computation.31.clone.1 | loop fusion | bytes 1048580 | tf_op jit(solution)/shard_map/while/body/jit(dynamic_index_in_dim)/dynamic_slice | solution.py:160
  44.4 0.1 squeeze.31
  44.5 0.1 squeeze.32
  44.6 1.1 %broadcast_select_fusion.4 = (bf16[4,128,2,1,128]{4,2,1,0,3:T(2,128)(2,1)S(1)}, bf16[4,128,2,1,128]{4,2,1,0,3:T(2,128)(2,1)S(1)}) fusion(bf16[4,128,2,1,128]{4,2,1,0,3:T(2,128)(2,1)S(1)} %squeeze.31, pred[4,128]{1,0:T(4,128)(4,1)S(1)} %add_compare_fusion.2, bf16[4,128,2,1,128]{4,2,1,0,3:T(2,128)(2,1)S(1)} %squeeze.32), kind=kLoop, calls=%fused_computation.25.clone.1 | loop fusion | flops 262144 | bytes 1049088 | tf_op jit(solution)/shard_map/while/body/eval_jaxpr/jit(_where)/select_n | solution.py:86
  45.7 0.7 pad_maximum_fusion.3
  46.4 0.4 copy.55
  46.9 0.6 gather_fusion
  47.6 0.2 select_select_fusion.2
  47.7 9.3 %conditional.3 = ((f32[2,8,256]{2,1,0:T(8,128)S(1)}, f32[2,8,256]{2,1,0:T(8,128)S(1)}, f32[2,8,256,128]{3,2,1,0:T(8,128)})) conditional(s32[]{:T(128)} %convert_element_type.41, (f32[2,8,256]{2,1,0:T(8,128)S(1)}, f32[2,8,256]{2,1,0:T(8,128)S(1)}, f32[2,8,256,128]{3,2,1,0:T(8,128)}) %tuple.63, (s32[]{:T(128)}, s32[]{:T(128)}, s32[]{:T(128)}, ...), branch_computations={%region_4.4_spmd, %region_5.7_spmd} | conditional | flops 1102325504 | bytes 49553512 | solution.py:140
  47.7 0.7 broadcast_compare_fusion
  48.4 0.2 compare_and_fusion
  48.6 0.1 reshape.144
  48.7 0.1 reshape.145
  48.8 0.0 copy-start
  48.8 1.4 %fusion.2 = (f32[2,8,256]{2,1,0:T(8,128)S(1)}, f32[2,512,256,8]{2,1,3,0:T(8,128)S(1)}) fusion(pred[256,512]{0,1:T(8,128)(4,1)S(1)} %compare_and_fusion, bf16[256,2,8,128]{3,0,2,1:T(8,128)(2,1)S(1)} %get-tuple-element.235, bf16[512,2,128,1]{2,1,0,3:T(2,128)(2,1)S(1)} %bitcast.45), kind=kOutput, calls=%fused_computation.4 | convolution fusion | flops 543158272 | bytes 9846784 | tf_op jit(solution)/shard_map/while/body/eval_jaxpr/cond/branch_1_fun/rkgd,pkd->kgrp/dot_general | solution.py:27
  50.2 2.0 %fusion.4 = f32[2,8,256]{2,1,0:T(8,128)S(1)} fusion(f32[2,512,256,8]{2,1,3,0:T(8,128)S(1)} %get-tuple-element.398, f32[2,8,256]{2,1,0:T(8,128)S(1)} %max.6, pred[256,512]{0,1:T(8,128)(4,1)S(1)} %compare_and_fusion), kind=kLoop, calls=%fused_computation.6 | loop fusion | flops 10481664 | bytes 8552448 | tf_op jit(solution)/shard_map/while/body/eval_jaxpr/cond/branch_1_fun/reduce_sum | solution.py:38
  52.2 0.0 copy-done
  52.3 3.4 %multiply_add_fusion = f32[2,8,256,128]{3,2,1,0:T(8,128)S(1)} fusion(f32[2,8,256,128]{3,2,1,0:T(8,128)S(1)} %copy-done, f32[2,512,256,8]{2,1,3,0:T(8,128)S(1)} %get-tuple-element.398, f32[2,8,256]{2,1,0:T(8,128)S(1)} %max.6, pred[256,512]{0,1:T(8,128)(4,1)S(1)} %compare_and_fusion, f32[2,8,256]{2,1,0:T(8,128)S(1)} %get-tuple-element.396, ...), kind=kOutput, calls=%fused_computation.9 | convolution fusion | flops 548405248 | bytes 13008896 | tf_op jit(solution)/shard_map/while/body/eval_jaxpr/cond/branch_1_fun/kgrp,pkd->kgrd/dot_general | solution.py:39
  55.7 0.0 copy-start.1
  55.7 1.3 %copy-done.1 = f32[2,8,256,128]{3,2,1,0:T(8,128)} copy-done((f32[2,8,256,128]{3,2,1,0:T(8,128)}, f32[2,8,256,128]{3,2,1,0:T(8,128)S(1)}, u32[]{:S(2)}) %copy-start.1) | copy-done | bytes 2097176 | tf_op jit(solution)/shard_map/while/body/eval_jaxpr/cond
  57.0 0.6 dynamic_slice.31
  58.3 0.7 add_compare_fusion.2
  59.0 1.1 %constant_dynamic-slice_fusion.3 = (bf16[1,512,256]{2,1,0:T(8,128)(2,1)S(1)}, bf16[1,512,256]{2,1,0:T(8,128)(2,1)S(1)}) fusion(bf16[2,512,256]{2,1,0:T(8,128)(2,1)} %get-tuple-element.558, s32[]{:T(128)S(6)} %copy.67, bf16[2,512,256]{2,1,0:T(8,128)(2,1)} %get-tuple-element.557), kind=kLoop, calls=%fused_computation.31.clone.1 | loop fusion | bytes 1048580 | tf_op jit(solution)/shard_map/while/body/jit(dynamic_index_in_dim)/dynamic_slice | solution.py:160
  60.1 0.1 squeeze.31
  60.2 0.1 squeeze.32
  60.2 1.1 %broadcast_select_fusion.4 = (bf16[4,128,2,1,128]{4,2,1,0,3:T(2,128)(2,1)S(1)}, bf16[4,128,2,1,128]{4,2,1,0,3:T(2,128)(2,1)S(1)}) fusion(bf16[4,128,2,1,128]{4,2,1,0,3:T(2,128)(2,1)S(1)} %squeeze.31, pred[4,128]{1,0:T(4,128)(4,1)S(1)} %add_compare_fusion.2, bf16[4,128,2,1,128]{4,2,1,0,3:T(2,128)(2,1)S(1)} %squeeze.32), kind=kLoop, calls=%fused_computation.25.clone.1 | loop fusion | flops 262144 | bytes 1049088 | tf_op jit(solution)/shard_map/while/body/eval_jaxpr/jit(_where)/select_n | solution.py:86
  61.4 0.7 pad_maximum_fusion.3
  62.1 0.4 copy.55
  62.6 0.6 gather_fusion
  63.2 0.2 select_select_fusion.2
  63.4 9.3 %conditional.3 = ((f32[2,8,256]{2,1,0:T(8,128)S(1)}, f32[2,8,256]{2,1,0:T(8,128)S(1)}, f32[2,8,256,128]{3,2,1,0:T(8,128)})) conditional(s32[]{:T(128)} %convert_element_type.41, (f32[2,8,256]{2,1,0:T(8,128)S(1)}, f32[2,8,256]{2,1,0:T(8,128)S(1)}, f32[2,8,256,128]{3,2,1,0:T(8,128)}) %tuple.63, (s32[]{:T(128)}, s32[]{:T(128)}, s32[]{:T(128)}, ...), branch_computations={%region_4.4_spmd, %region_5.7_spmd} | conditional | flops 1102325504 | bytes 49553512 | solution.py:140
  63.4 0.7 broadcast_compare_fusion
  64.1 0.2 compare_and_fusion
  64.3 0.1 reshape.144
  64.4 0.1 reshape.145
  64.4 0.0 copy-start
  64.4 1.4 %fusion.2 = (f32[2,8,256]{2,1,0:T(8,128)S(1)}, f32[2,512,256,8]{2,1,3,0:T(8,128)S(1)}) fusion(pred[256,512]{0,1:T(8,128)(4,1)S(1)} %compare_and_fusion, bf16[256,2,8,128]{3,0,2,1:T(8,128)(2,1)S(1)} %get-tuple-element.235, bf16[512,2,128,1]{2,1,0,3:T(2,128)(2,1)S(1)} %bitcast.45), kind=kOutput, calls=%fused_computation.4 | convolution fusion | flops 543158272 | bytes 9846784 | tf_op jit(solution)/shard_map/while/body/eval_jaxpr/cond/branch_1_fun/rkgd,pkd->kgrp/dot_general | solution.py:27
  65.9 2.0 %fusion.4 = f32[2,8,256]{2,1,0:T(8,128)S(1)} fusion(f32[2,512,256,8]{2,1,3,0:T(8,128)S(1)} %get-tuple-element.398, f32[2,8,256]{2,1,0:T(8,128)S(1)} %max.6, pred[256,512]{0,1:T(8,128)(4,1)S(1)} %compare_and_fusion), kind=kLoop, calls=%fused_computation.6 | loop fusion | flops 10481664 | bytes 8552448 | tf_op jit(solution)/shard_map/while/body/eval_jaxpr/cond/branch_1_fun/reduce_sum | solution.py:38
  67.9 0.0 copy-done
  67.9 3.4 %multiply_add_fusion = f32[2,8,256,128]{3,2,1,0:T(8,128)S(1)} fusion(f32[2,8,256,128]{3,2,1,0:T(8,128)S(1)} %copy-done, f32[2,512,256,8]{2,1,3,0:T(8,128)S(1)} %get-tuple-element.398, f32[2,8,256]{2,1,0:T(8,128)S(1)} %max.6, pred[256,512]{0,1:T(8,128)(4,1)S(1)} %compare_and_fusion, f32[2,8,256]{2,1,0:T(8,128)S(1)} %get-tuple-element.396, ...), kind=kOutput, calls=%fused_computation.9 | convolution fusion | flops 548405248 | bytes 13008896 | tf_op jit(solution)/shard_map/while/body/eval_jaxpr/cond/branch_1_fun/kgrp,pkd->kgrd/dot_general | solution.py:39
  71.3 0.0 copy-start.1
  71.3 1.3 %copy-done.1 = f32[2,8,256,128]{3,2,1,0:T(8,128)} copy-done((f32[2,8,256,128]{3,2,1,0:T(8,128)}, f32[2,8,256,128]{3,2,1,0:T(8,128)S(1)}, u32[]{:S(2)}) %copy-start.1) | copy-done | bytes 2097176 | tf_op jit(solution)/shard_map/while/body/eval_jaxpr/cond
  72.7 2.0 %fusion.17 = bf16[256,2,8,128]{3,0,2,1:T(8,128)(2,1)S(1)} fusion(f32[2,8,256,128]{3,2,1,0:T(8,128)} %get-tuple-element.262, f32[2,8,256]{2,1,0:T(8,128)S(1)} %broadcast_select_fusion.2, pred[256]{0:T(512)(128)(4,1)S(1)} %broadcast_compare_fusion.1), kind=kLoop, calls=%fused_computation.35 | loop fusion | flops 1572864 | bytes 3162368 | tf_op jit(solution)/shard_map/convert_element_type | solution.py:53
  74.7 0.7 copy.36
  75.4 1.2 %copy.53 = bf16[32,8,16,128]{3,1,2,0:T(8,128)(2,1)} copy(bf16[32,8,16,128]{3,2,1,0:T(8,128)(2,1)S(1)} %bitcast.47) | data formatting | bytes 2097152
  76.6 1.0 %copy.37 = bf16[4,128,512]{2,1,0:T(8,128)(2,1)} copy(bf16[4,128,512]{1,2,0:T(8,128)(2,1)S(1)} %get-tuple-element.363) | data formatting | bytes 1048576
  (26 shorter events, 0.1 us)
Async XLA Ops:
  7.2 30.4 %all-gather.2.cloned.1.call-start = ((), (), s32[]{:S(2)}) async-start(), calls=%async_computation | async-start | bytes 1310720 | tf_op jit(solution)/shard_map/all_gather | solution.py:119
  48.8 3.5 %copy-start = (f32[2,8,256,128]{3,2,1,0:T(8,128)S(1)}, f32[2,8,256,128]{3,2,1,0:T(8,128)}, u32[]{:S(2)}) copy-start(f32[2,8,256,128]{3,2,1,0:T(8,128)} %get-tuple-element.237) | copy-start | bytes 6291460 | tf_op jit(solution)/shard_map/while/body/eval_jaxpr/cond
  55.7 1.4 %copy-start.1 = (f32[2,8,256,128]{3,2,1,0:T(8,128)}, f32[2,8,256,128]{3,2,1,0:T(8,128)S(1)}, u32[]{:S(2)}) copy-start(f32[2,8,256,128]{3,2,1,0:T(8,128)S(1)} %multiply_add_fusion) | copy-start | bytes 6291460 | tf_op jit(solution)/shard_map/while/body/eval_jaxpr/cond
  64.4 3.5 %copy-start = (f32[2,8,256,128]{3,2,1,0:T(8,128)S(1)}, f32[2,8,256,128]{3,2,1,0:T(8,128)}, u32[]{:S(2)}) copy-start(f32[2,8,256,128]{3,2,1,0:T(8,128)} %get-tuple-element.237) | copy-start | bytes 6291460 | tf_op jit(solution)/shard_map/while/body/eval_jaxpr/cond
  71.3 1.4 %copy-start.1 = (f32[2,8,256,128]{3,2,1,0:T(8,128)}, f32[2,8,256,128]{3,2,1,0:T(8,128)S(1)}, u32[]{:S(2)}) copy-start(f32[2,8,256,128]{3,2,1,0:T(8,128)S(1)} %multiply_add_fusion) | copy-start | bytes 6291460 | tf_op jit(solution)/shard_map/while/body/eval_jaxpr/cond
Sparse Core Ops, SparseCore 0:
  10.1 27.3 all-gather.1
